TPU v7x, 512 devices: a whole 4x4x16 slice. The times are simulated.
512 devices in a mesh: lat: 32 (over z, x_hi), lon: 16 (over y, x_lo, core).
Axes of the slice: x: 4 (x_hi: 2, x_lo: 2; x = x_hi * 2 + x_lo), y: 4, z: 16, core: 2. Of those that a mesh axis runs over, the one named last changes fastest.
Arguments:
- fields: float32 [8, 32, 512, 2048], P(None, None, 'lat', 'lon'), may hold values from -6 to 6
- ocean_mask: int32 [512, 16], replicated, may hold values from 0 to 1, as said below
- scale_table: float32 [16], replicated, may hold values from 0.5 to 4
- offset_table: float32 [16], replicated, may hold values from -4 to 4
- scale_index: int32 [8], replicated, may hold values from 0 to 15
- offset_index: int32 [8], replicated, may hold values from 0 to 15
Outputs:
- history: float32 [8, 32, 512, 2048], P(None, 'lat', 'lon')
- record_range: float32 [2, 8, 32], P(None, None, 'lat')
Inputs may be any that keep to these rules, and one draw needn't show every extreme that they name: `ocean_mask`: each device's block of 16 rows and 128 longitudes holds at least half of 12 (rounded down, and never fewer than one) and at most 12 ocean strips; some block holds exactly 12.
All inputs are finite; a program needn't handle non-finite values.
Results may differ from a plain program's by a relative error of at most 0.00007.
Values sent between devices are 32-bit elements; how exact they have to be, the bound alone decides.
A program may use at most 64 MiB of HBM per device.

v0:
```python
import jax
import jax.numpy as jnp
from jax import lax
from jax.sharding import PartitionSpec as P

STRIP = 128
MAX_LIVE = 12


def copy_for_each(x, axis):
    copies = jnp.broadcast_to(x, (lax.axis_size(axis), *x.shape))
    return lax.all_to_all(copies, axis, split_axis=0, concat_axis=0, tiled=True)


def taken_together(x, axis):
    return copy_for_each(x, axis).max(axis=0)


def per_device(fields, ocean_mask, scale_table, offset_table, scale_index, offset_index):
    nfield, level_count, lat_rows, lon_cells = fields.shape
    lat_count = lax.axis_size("lat")
    lon_count = lax.axis_size("lon")
    lat_pos = lax.axis_index("lat")
    lon_pos = lax.axis_index("lon")
    strips = lon_cells // STRIP
    strips_dev = lat_rows * strips
    slab_blocks = lat_count // lon_count
    levels_own = level_count // lat_count
    table_slots = jnp.arange(scale_table.shape[0])
    scale_pick = scale_index[:, None] == table_slots[None, :]
    offset_pick = offset_index[:, None] == table_slots[None, :]
    scales = jnp.sum(jnp.where(scale_pick, scale_table[None, :], 0.0), axis=1)
    offsets = jnp.sum(jnp.where(offset_pick, offset_table[None, :], 0.0), axis=1)
    own_mask = lax.dynamic_slice(
        ocean_mask, (lat_pos * lat_rows, lon_pos * strips), (lat_rows, strips)
    )
    packed = (fields - offsets[:, None, None, None]) * scales[:, None, None, None]
    slab_mask = lax.dynamic_slice(
        ocean_mask,
        (lon_pos * slab_blocks * lat_rows, 0),
        (slab_blocks * lat_rows, lon_count * strips),
    )
    slab_live = jnp.repeat(slab_mask, STRIP, axis=1) > 0
    flat_live = own_mask.reshape(-1)
    order_key = (1 - flat_live) * strips_dev + jnp.arange(strips_dev, dtype=jnp.int32)
    chosen = jnp.argsort(order_key)[:MAX_LIVE]
    kept_flag = flat_live[chosen] > 0
    compact = jnp.take(packed, chosen, axis=2)
    compact = jnp.where(kept_flag[None, None, :, None], compact, 0.0)
    arrived = lax.all_to_all(
        lax.all_to_all(compact, "lat", split_axis=1, concat_axis=2, tiled=True),
        "lon",
        split_axis=2,
        concat_axis=3,
        tiled=True,
    )
    arrived = arrived.reshape(nfield, levels_own, slab_blocks, MAX_LIVE, lon_count, STRIP)
    block_mask = slab_mask.reshape(slab_blocks, lat_rows, lon_count, strips).transpose(0, 2, 1, 3)
    block_mask = block_mask.reshape(slab_blocks, lon_count, strips_dev)
    strip_rank = jnp.cumsum(block_mask, axis=2) - 1
    slot_ids = jnp.arange(MAX_LIVE, dtype=jnp.int32)
    selector = (strip_rank[:, :, :, None] == slot_ids[None, None, None, :]) & (
        block_mask[:, :, :, None] > 0
    )
    selector = selector.astype(jnp.float32).transpose(0, 2, 1, 3)
    picked = jnp.einsum("bsjk,flbkjc->flbsjc", selector, arrived, precision=lax.Precision.HIGHEST)
    picked = picked.reshape(nfield, levels_own, slab_blocks, lat_rows, strips, lon_count, STRIP)
    picked = picked.transpose(0, 1, 2, 3, 5, 4, 6)
    history = picked.reshape(nfield, levels_own, slab_blocks * lat_rows, lon_count * strips * STRIP)
    highest = jnp.max(jnp.where(slab_live[None, None], history, -jnp.inf), axis=(2, 3))
    negated = jnp.max(jnp.where(slab_live[None, None], -history, -jnp.inf), axis=(2, 3))
    own_levels = taken_together(jnp.stack([highest, negated]), "lon")
    record_range = jnp.stack([own_levels[0], -own_levels[1]])
    return (history, record_range)


def solution(mesh):
    return jax.shard_map(
        per_device,
        mesh=mesh,
        in_specs=(P(None, None, "lat", "lon"), P(), P(), P(), P(), P()),
        out_specs=(P(None, "lat", "lon", None), P(None, None, "lat")),
        check_vma=False,
    )
```

profile of v0, /device:TPU:1, one launch (start us, length us, event | category | flops | bytes accessed | tf_op | source)
XLA Modules:
  0.0 148.9 jit_solution(1912339024605151337)
XLA Ops:
  0.6 0.8 iota_add_fusion
  1.4 1.2 sort.17
  2.7 0.7 gather_fusion
  3.3 0.9 select_reduce_fusion.2
  4.3 3.6 %fusion.2 = f32[8,32,16,128]{3,1,2,0:T(8,128)} fusion(f32[8,32,16,128]{3,2,1,0:T(8,128)} %param.6, f32[8]{0:T(128)S(1)} %get-tuple-element.21, f32[8]{0:T(128)S(1)} %get-tuple-element.22), kind=kLoop, calls=%fused_computation.5 | loop fusion | flops 1048576 | bytes 4194368 | tf_op jit(solution)/shard_map/mul | solution.py:37
  7.9 2.2 %gather_fusion.1 = f32[12,8,32,128]{3,2,1,0:T(8,128)S(1)} fusion(f32[8,32,16,128]{3,1,2,0:T(8,128)} %fusion.2, s32[1024]{0:T(1024)S(1)} %pad_clamp_fusion), kind=kCustom, calls=%fused_computation.1 | custom fusion | bytes 3145776 | tf_op jit(solution)/shard_map/jit(_take)/gather | solution.py:48
  10.1 0.3 select_bitcast_fusion
  10.5 0.9 copy.45
  11.4 94.6 %all_to_all.32 = f32[8,32,12,128]{3,0,2,1:T(8,128)} all-to-all(f32[8,32,12,128]{3,0,2,1:T(8,128)S(1)} %copy.45), channel_id=1, replica_groups=mesh['lat'=32,'lon'=16] {'lat'}, dimensions={1} | all-to-all | bytes 3145728 | tf_op jit(solution)/shard_map/all_to_all | solution.py:51
  106.0 7.1 %all-to-all-start.1 = ((f32[8,1,384,128]{3,0,1,2:T(8,128)}), f32[8,1,384,128]{3,0,1,2:T(8,128)S(1)}, u32[]{:S(2)}, u32[]{:S(2)}) async-start(f32[8,1,384,128]{3,0,1,2:T(8,128)} %bitcast.3), calls=%async_computation.1 | async-start | bytes 3145728 | tf_op jit(solution)/shard_map/all_to_all | solution.py:50
  113.1 0.8 constant_dynamic-slice_fusion
  113.9 0.1 copy.59
  114.0 0.1 copy.55
  114.1 0.1 copy.58
  114.2 0.4 reduce_window_sum.14
  114.5 19.9 %all-to-all-done.1 = f32[8,1,384,128]{3,0,1,2:T(8,128)S(1)} async-done(((f32[8,1,384,128]{3,0,1,2:T(8,128)}), f32[8,1,384,128]{3,0,1,2:T(8,128)S(1)}, u32[]{:S(2)}, u32[]{:S(2)}) %all-to-all-start.1) | async-done | bytes 1572896 | tf_op jit(solution)/shard_map/all_to_all | solution.py:50
  134.4 0.3 copy.47
  134.7 0.3 copy.48
  135.0 2.6 %select_reduce_fusion.1 = (f32[8]{0:T(128)S(1)}, f32[8]{0:T(128)S(1)}, f32[8,1,2,16,16,128]{5,3,0,4,2,1:T(8,128)S(1)}) fusion(pred[2,16,16]{1,2,0:T(8,128)(4,1)S(1)} %copy.55, s32[2,16,16]{1,2,0:T(8,128)S(1)} %add_bitcast_fusion, pred[2,16,16]{1,2,0:T(8,128)(4,1)S(1)} %copy.52, f32[8,2,12,16,128]{4,3,2,1,0:T(8,128)S(1)} %bitcast.45), kind=kOutput, calls=%fused_computation.7 | convolution fusion | flops 78131184 | bytes 3673152 | tf_op jit(solution)/shard_map/bsjk,flbkjc->flbsjc/dot_general | solution.py:66
  137.6 0.6 broadcast_in_dim.86
  138.2 4.3 %all-to-all-start.2 = ((f32[16,2,8,1]{2,1,3,0:T(2,128)}), f32[16,2,8,1]{2,1,3,0:T(2,128)S(1)}, u32[]{:S(2)}, u32[]{:S(2)}) async-start(f32[16,2,8,1]{2,1,3,0:T(2,128)} %broadcast_in_dim.86), calls=%async_computation.2 | async-start | bytes 32768 | tf_op jit(solution)/shard_map/all_to_all | solution.py:12
  142.5 1.2 copy.54
  143.7 2.2 %copy.56 = f32[8,1,32,2048]{3,2,1,0:T(8,128)} copy(f32[8,1,32,2048]{3,1,2,0:T(1,128)S(1)} %bitcast.43) | data formatting | bytes 4194304
  145.9 2.4 %all-to-all-done.2 = f32[16,2,8,1]{2,1,3,0:T(2,128)S(1)} async-done(((f32[16,2,8,1]{2,1,3,0:T(2,128)}), f32[16,2,8,1]{2,1,3,0:T(2,128)S(1)}, u32[]{:S(2)}, u32[]{:S(2)}) %all-to-all-start.2) | async-done | bytes 1056 | tf_op jit(solution)/shard_map/all_to_all | solution.py:12
  148.4 0.6 pad_maximum_fusion.1
  (12 shorter events, 0.1 us)
Async XLA Ops:
  106.0 28.4 %all-to-all-start.1 = ((f32[8,1,384,128]{3,0,1,2:T(8,128)}), f32[8,1,384,128]{3,0,1,2:T(8,128)S(1)}, u32[]{:S(2)}, u32[]{:S(2)}) async-start(f32[8,1,384,128]{3,0,1,2:T(8,128)} %bitcast.3), calls=%async_computation.1 | async-start | bytes 3145728 | tf_op jit(solution)/shard_map/all_to_all | solution.py:50
  138.2 10.1 %all-to-all-start.2 = ((f32[16,2,8,1]{2,1,3,0:T(2,128)}), f32[16,2,8,1]{2,1,3,0:T(2,128)S(1)}, u32[]{:S(2)}, u32[]{:S(2)}) async-start(f32[16,2,8,1]{2,1,3,0:T(2,128)} %broadcast_in_dim.86), calls=%async_computation.2 | async-start | bytes 32768 | tf_op jit(solution)/shard_map/all_to_all | solution.py:12
where the time goes:
time: 149 us
  blocking collectives  94.6 us (63%)
  waiting for transfers between devices  22.3 us (15%)
  starting transfers between devices  11.4 us (8%)
  local copies, waits for them, and re-layouts  9.43 us (6%)
  other arithmetic  7.9 us (5%)
  matrix products  2.57 us (2%)
    all_to_all x1, blocking collectives, per_device(): lax.all_to_all(compact, 'lat', split_axis=1, concat_axis=2, tiled=True)  94.6 us
    all_to_all x1, waiting for transfers between devices, per_device(): lax.all_to_all(lax.all_to_all(compact, 'lat', split_axis=1, concat_axis=2...  19.9 us
    all_to_all x1, starting transfers between devices, per_device(): lax.all_to_all(lax.all_to_all(compact, 'lat', split_axis=1, concat_axis=2...  7.12 us
    all_to_all x1, starting transfers between devices, copy_for_each(): return lax.all_to_all(copies, axis, split_axis=0, concat_axis=0, tiled=True)  4.25 us
    mul x1, other arithmetic, per_device(): (fields - offsets[:, None, None, None]) * scales[:, None, None, None]  3.64 us
  transfers between devices with their start and end apart: 2, of which 2 were waited for; matrix products, arithmetic and copies ran while one was open for 3% of the time, Pallas kernels for 0%

commit v1 on v0

v1 whole, which is shorter than its diff:
```python
import functools

import jax
import jax.numpy as jnp
from jax import lax
from jax.experimental import pallas as pl
from jax.experimental.pallas import tpu as pltpu
from jax.sharding import PartitionSpec as P

MESH = pl.DeviceIdType.MESH
FIELDS = 8
LEVELS = 32
ROWS = 16
LANES = 128
SLOTS = 12
PLANES = 16
LONS = 16
SENDERS = 32
FIELD_STRIDE = LEVELS * ROWS + 8
OUT_STRIDE = 2 * ROWS * LONS
STEPS = PLANES // 2
LAG = 2
STRIDE = 3

def remote(src, dst, send_sem, recv_sem, device):
    return pltpu.make_async_remote_copy(
        src_ref=src, dst_ref=dst, send_sem=send_sem, recv_sem=recv_sem,
        device_id=device, device_id_type=MESH,
    )


def kernel(
    scale_hbm, offset_hbm, scale_index_hbm, offset_index_hbm, fields, mask,
    out, range_out,
    scale_table, offset_table, scale_index, offset_index, staged, own_mask, slab_mask, packed, passing, arrived, block, spread_out,
    stat, stat_in, part, part_in, total, range_in,
    load_sem, mask_sem, table_sem, column_send, column_recv,
    send_sem, recv_sem, stat_send, stat_recv, part_send, part_recv, range_send, range_recv, out_sem,
):
    lat = lax.axis_index("lat")
    lon = lax.axis_index("lon")
    plane = lat // 2
    half = lat % 2
    me = half * LONS + lon
    barrier = pltpu.get_barrier_semaphore()

    def at_plane(offset):
        return (lax.rem(plane + offset + PLANES, PLANES) * 2 + half, lon)

    def in_plane(i):
        return (plane * 2 + i // LONS, lax.rem(i, LONS))

    def signal_column(k, carry):
        pl.semaphore_signal(barrier, inc=1, device_id=at_plane(k), device_id_type=MESH)
        return carry

    def signal_plane(k, carry):
        pl.semaphore_signal(
            barrier, inc=1, device_id=in_plane(lax.rem(me + k, SENDERS)), device_id_type=MESH
        )
        return carry

    lax.fori_loop(1, PLANES, signal_column, 0)
    lax.fori_loop(1, SENDERS, signal_plane, 0)

    own_column = pl.multiple_of((lat // 8) * LANES, LANES)
    slab_column = pl.multiple_of((lon // 4) * LANES, LANES)
    own_load = pltpu.make_async_copy(
        mask.at[:, pl.ds(own_column, LANES)], own_mask, mask_sem.at[0]
    )
    slab_load = pltpu.make_async_copy(
        mask.at[:, pl.ds(slab_column, LANES)], slab_mask, mask_sem.at[1]
    )
    own_load.start()
    slab_load.start()
    table_loads = [
        pltpu.make_async_copy(src, dst, table_sem.at[i])
        for i, (src, dst) in enumerate((
            (scale_hbm, scale_table), (offset_hbm, offset_table),
            (scale_index_hbm, scale_index), (offset_index_hbm, offset_index),
        ))
    ]
    for load in table_loads:
        load.start()
    loads = [
        pltpu.make_async_copy(
            fields.at[f], staged.at[pl.ds(f * FIELD_STRIDE, LEVELS * ROWS)], load_sem.at[f]
        )
        for f in range(FIELDS)
    ]
    for load in loads:
        load.start()

    for load in table_loads:
        load.wait()
    field_row = lax.broadcasted_iota(jnp.int32, (FIELDS, LANES), 0)
    lane = lax.broadcasted_iota(jnp.int32, (FIELDS, LANES), 1)
    scales = jnp.zeros((FIELDS, LANES), jnp.float32)
    offsets = jnp.zeros((FIELDS, LANES), jnp.float32)
    for f in range(FIELDS):
        scales = jnp.where(field_row == f, scale_table[scale_index[f]], scales)
        offsets = jnp.where(field_row == f, offset_table[offset_index[f]], offsets)

    own_load.wait()
    first = (lat % 8) * ROWS
    live = [own_mask[lon, first + s] for s in range(ROWS)]
    chosen = [jnp.int32(0)] * SLOTS
    count = jnp.int32(0)
    for s in range(ROWS):
        for k in range(SLOTS):
            if k <= s:
                chosen[k] = jnp.where((live[s] > 0) & (count == k), s, chosen[k])
        count = count + live[s]
    for k in range(1, SLOTS):
        chosen[k] = jnp.where(k < count, chosen[k], chosen[0])

    for load in loads:
        load.wait()

    def pack(level, carry):
        base = level * ROWS
        highest = None
        lowest = None
        for k in range(SLOTS):
            rows = staged[pl.ds(base + chosen[k], FIELDS, stride=FIELD_STRIDE), :]
            value = (rows - offsets) * scales
            packed[level, k] = value
            highest = value if k == 0 else jnp.maximum(highest, value)
            lowest = value if k == 0 else jnp.minimum(lowest, value)
        high = jnp.max(highest, axis=1, keepdims=True)
        low = jnp.max(-lowest, axis=1, keepdims=True)
        spread = jnp.where(
            lane == field_row, high, jnp.where(lane == field_row + FIELDS, low, -jnp.inf)
        )
        stat[level] = jnp.max(spread, axis=0, keepdims=True)
        return carry

    lax.fori_loop(0, LEVELS, pack, 0)

    pl.semaphore_wait(barrier, PLANES + SENDERS - 2)

    turn = lon // 2

    def distance(step):
        return 1 + lax.rem(STRIDE * step + turn, STEPS)

    def column_copy(step, sign):
        offset = distance(step) * (1 - 2 * sign)
        level = pl.multiple_of(lax.rem(plane + offset + PLANES, PLANES) * 2, 2)
        return remote(
            packed.at[pl.ds(level, 2)], passing.at[step, sign],
            column_send.at[step, sign], column_recv.at[step, sign], at_plane(offset),
        )

    def both_signs(step, act):
        act(0)

        @pl.when(distance(step) < STEPS)
        def _():
            act(1)

    def hand_on(source, slot, origin):
        for h in range(2):
            mine = (origin == lon) & (half == h)

            @pl.when(jnp.logical_not(mine))
            def _():
                remote(
                    source(h), arrived.at[me], send_sem.at[slot, h], recv_sem.at[me],
                    (plane * 2 + h, origin),
                ).start()

            @pl.when(mine)
            def _():
                for k in range(SLOTS):
                    arrived[me, k] = source(h)[k]

    def handed_on(source, slot, origin):
        for h in range(2):
            @pl.when(jnp.logical_not((origin == lon) & (half == h)))
            def _():
                remote(
                    source(h), arrived.at[0], send_sem.at[slot, h], recv_sem.at[0], (lat, lon)
                ).wait_send()

    def send_stat(k, carry):
        level = lax.rem(me + k, SENDERS)
        remote(
            stat.at[level], stat_in.at[me], stat_send.at[level], stat_recv.at[me], in_plane(level)
        ).start()
        return carry

    lax.fori_loop(1, SENDERS, send_stat, 0)
    stat_in[me] = stat[me]

    def start_column(step, carry):
        both_signs(step, lambda sign: column_copy(step, sign).start())
        return carry

    lax.fori_loop(0, STEPS, start_column, 0)
    hand_on(lambda h: packed.at[plane * 2 + h], 2 * STEPS, plane)

    def take_stat(k, best):
        i = lax.rem(me + k, SENDERS)
        remote(stat.at[0], stat_in.at[i], stat_send.at[i], stat_recv.at[i], (lat, lon)).wait_recv()
        return jnp.maximum(best, stat_in[i])

    best = lax.fori_loop(1, SENDERS, take_stat, stat_in[me])
    part[...] = best
    for k in range(1, PLANES):
        remote(part, part_in.at[k], part_send.at[k], part_recv.at[k], at_plane(k)).start()

    slab_load.wait()
    slab_first = (lon % 4) * 2 * ROWS

    def unpack(i):
        h = i // LONS
        q = lax.rem(i, LONS)

        @pl.when(i != me)
        def _():
            remote(
                packed.at[0], arrived.at[i], send_sem.at[0, 0], recv_sem.at[i], (lat, lon)
            ).wait_recv()

        for k in range(SLOTS):
            block[k] = arrived[i, k]
        rank = jnp.int32(0)
        for s in range(ROWS):
            wet = slab_mask[q, slab_first + h * ROWS + s]
            value = block[jnp.minimum(rank, SLOTS - 1)]
            rank = rank + wet
            row = (h * 2 + s // 8) * (LONS * 8) + q * 8 + s % 8
            spread_out[pl.ds(row, FIELDS, stride=OUT_STRIDE), :] = jnp.where(wet > 0, value, 0.0)

    away = lax.rem(plane - lon + PLANES, PLANES)
    away = jnp.where(away > STEPS, PLANES - away, away)

    def unpack_step(step):
        column = lax.rem(away - 1 - STRIDE * step + 8 * STEPS, STEPS) * 2
        for h in range(2):
            for c in range(2):
                unpack(h * LONS + column + c)

    def relay(step, carry):
        def pass_on(sign):
            column_copy(step, sign).wait_recv()
            origin = lax.rem(plane - distance(step) * (1 - 2 * sign) + PLANES, PLANES)
            hand_on(lambda h: passing.at[step, sign, h], 2 * step + sign, origin)

        both_signs(step, pass_on)

        @pl.when(step >= LAG)
        def _():
            unpack_step(step - LAG)
        return carry

    lax.fori_loop(0, STEPS, relay, 0)

    best = part[...]
    for k in range(1, PLANES):
        remote(part, part_in.at[k], part_send.at[k], part_recv.at[k], (lat, lon)).wait_recv()
        best = jnp.maximum(best, part_in[k])
    total[...] = best
    tells = me // 2 == plane

    def range_copy(q):
        return remote(
            total, range_in, range_send.at[q], range_recv, (plane * 2 + lax.rem(me, 2), q)
        )

    def told_self(q):
        return (q == lon) & (lax.rem(me, 2) == half)

    def tell(q, carry):
        @pl.when(tells & jnp.logical_not(told_self(q)))
        def _():
            range_copy(q).start()

        @pl.when(tells & told_self(q))
        def _():
            range_in[...] = total[...]
        return carry

    lax.fori_loop(0, LONS, tell, 0)

    def unpack_rest(step, carry):
        unpack_step(step)
        return carry

    lax.fori_loop(STEPS - LAG, STEPS, unpack_rest, 0)
    stores = [
        pltpu.make_async_copy(
            spread_out.at[pl.ds(f * OUT_STRIDE, OUT_STRIDE)], out.at[f], out_sem.at[f]
        )
        for f in range(FIELDS)
    ]
    for store in stores:
        store.start()

    @pl.when(jnp.logical_not((lat == me)))
    def _():
        remote(total, range_in, range_send.at[0], range_recv, (lat, lon)).wait_recv()

    range_out[...] = range_in[...]

    def told(q, carry):
        @pl.when(tells & jnp.logical_not(told_self(q)))
        def _():
            range_copy(q).wait_send()
        return carry

    lax.fori_loop(0, LONS, told, 0)

    def drain_stat(k, carry):
        level = lax.rem(me + k, SENDERS)
        remote(
            stat.at[level], stat_in.at[0], stat_send.at[level], stat_recv.at[0], (lat, lon)
        ).wait_send()
        return carry

    lax.fori_loop(1, SENDERS, drain_stat, 0)

    def drain(step, carry):
        def one(sign):
            column_copy(step, sign).wait_send()
            origin = lax.rem(plane - distance(step) * (1 - 2 * sign) + PLANES, PLANES)
            handed_on(lambda h: passing.at[step, sign, h], 2 * step + sign, origin)

        both_signs(step, one)
        return carry

    lax.fori_loop(0, STEPS, drain, 0)
    handed_on(lambda h: packed.at[plane * 2 + h], 2 * STEPS, plane)
    for k in range(1, PLANES):
        remote(part, part_in.at[k], part_send.at[k], part_recv.at[k], (lat, lon)).wait_send()
    for store in stores:
        store.wait()


def per_device(fields, ocean_mask, scale_table, offset_table, scale_index, offset_index):
    vmem = pl.BlockSpec(memory_space=pltpu.VMEM)
    hbm = pl.BlockSpec(memory_space=pltpu.HBM)
    dma = pltpu.SemaphoreType.DMA
    out, best = pl.pallas_call(
        kernel,
        name="exchange",
        out_shape=(
            jax.ShapeDtypeStruct((FIELDS, OUT_STRIDE, LANES), jnp.float32),
            jax.ShapeDtypeStruct((1, LANES), jnp.float32),
        ),
        in_specs=[hbm] * 6,
        out_specs=(hbm, vmem),
        scratch_shapes=[
            pltpu.SMEM((16,), jnp.float32), pltpu.SMEM((16,), jnp.float32),
            pltpu.SMEM((FIELDS,), jnp.int32), pltpu.SMEM((FIELDS,), jnp.int32),
            pltpu.VMEM((FIELDS * FIELD_STRIDE, LANES), jnp.float32),
            pltpu.SMEM((LONS, LANES), jnp.int32),
            pltpu.SMEM((LONS, LANES), jnp.int32),
            pltpu.VMEM((LEVELS, SLOTS, FIELDS, LANES), jnp.float32),
            pltpu.VMEM((STEPS, 2, 2, SLOTS, FIELDS, LANES), jnp.float32),
            pltpu.VMEM((SENDERS, SLOTS, FIELDS, LANES), jnp.float32),
            pltpu.VMEM((SLOTS, FIELDS, LANES), jnp.float32),
            pltpu.VMEM((FIELDS * OUT_STRIDE, LANES), jnp.float32),
            pltpu.VMEM((LEVELS, 1, LANES), jnp.float32),
            pltpu.VMEM((SENDERS, 1, LANES), jnp.float32),
            pltpu.VMEM((1, LANES), jnp.float32),
            pltpu.VMEM((PLANES, 1, LANES), jnp.float32),
            pltpu.VMEM((1, LANES), jnp.float32),
            pltpu.VMEM((1, LANES), jnp.float32),
            dma((FIELDS,)), dma((2,)), dma((4,)),
            dma((STEPS, 2)), dma((STEPS, 2)), dma((2 * STEPS + 1, 2)), dma((SENDERS,)),
            dma((LEVELS,)), dma((SENDERS,)), dma((PLANES,)), dma((PLANES,)),
            dma((LONS,)), dma, dma((FIELDS,)),
        ],
        compiler_params=pltpu.CompilerParams(
            collective_id=0, has_side_effects=True, vmem_limit_bytes=65472 * 1024
        ),
    )(
        scale_table, offset_table, scale_index, offset_index,
        fields.reshape(FIELDS, LEVELS * ROWS, LANES), ocean_mask.T,
    )
    history = out.reshape(FIELDS, 4, LONS, 8, LANES).transpose(0, 1, 3, 2, 4)
    history = history.reshape(FIELDS, 1, 2 * ROWS, LONS * LANES)
    record_range = jnp.stack([best[0, :FIELDS], -best[0, FIELDS:2 * FIELDS]])[:, :, None]
    return history, record_range


def solution(mesh):
    return jax.shard_map(
        per_device,
        mesh=mesh,
        in_specs=(P(None, None, "lat", "lon"), P(), P(), P(), P(), P()),
        out_specs=(P(None, "lat", "lon", None), P(None, None, "lat")),
        check_vma=False,
    )
```

time: 149 us -> 104 us (0.70)
  Pallas kernels: 0 us -> 97.8 us
  blocking collectives: 94.6 us -> 0 us
  waiting for transfers between devices: 22.3 us -> 0 us
  starting transfers between devices: 11.4 us -> 0 us
  other arithmetic: 7.9 us -> 1.33 us
  local copies, waits for them, and re-layouts: 9.43 us -> 3.13 us
  matrix products: 2.57 us -> 0 us
    pallas_call x0 -> x1, Pallas kernels: none -> 97.8 us  [per_device(): pl.pallas_call(kernel, name='exchange', out_shape=(jax.ShapeDtypeStruct((...]
    all_to_all x1 -> x0, blocking collectives: 94.6 us -> none  [per_device(): lax.all_to_all(compact, 'lat', split_axis=1, concat_axis=2, tiled=True)]
    all_to_all x2 -> x0, waiting for transfers between devices: 22.3 us -> none  [the longest x1 19.9 us: per_device(): lax.all_to_all(lax.all_to_all(compact, 'lat', split_axis=1, concat_axis=2...]
    all_to_all x2 -> x0, starting transfers between devices: 11.4 us -> none  [the longest x1 7.12 us: per_device(): lax.all_to_all(lax.all_to_all(compact, 'lat', split_axis=1, concat_axis=2...]
    mul x1 -> x0, other arithmetic: 3.64 us -> none  [per_device(): (fields - offsets[:, None, None, None]) * scales[:, None, None, None]]
    gather x2 -> x0, local copies, waits for them, and re-layouts: 2.89 us -> none  [the longest x1 2.24 us: per_device(): compact = jnp.take(packed, chosen, axis=2)]
    dot_general x1 -> x0, matrix products: 2.57 us -> none  [per_device(): jnp.einsum('bsjk,flbkjc->flbsjc', selector, arrived, precision=lax.Precis...]
    unnamed x2 -> x1, local copies, waits for them, and re-layouts: 2.27 us -> 3.13 us
  transfers between devices with their start and end apart: 2 -> 0, of which waited for: 2 -> 0; matrix products, arithmetic and copies ran while one was open for 3% -> 0% of each run, Pallas kernels for 0% -> 0%
where the time goes in v1:
time: 104 us; the launch traced here: 103 us
  Pallas kernels  97.8 us (94%)
  local copies, waits for them, and re-layouts  3.13 us (3%)
  other arithmetic  1.33 us (1%)
    pallas_call x1, Pallas kernels, per_device(): pl.pallas_call(kernel, name='exchange', out_shape=(jax.ShapeDtypeStruct((...  97.8 us
    unnamed x1, local copies, waits for them, and re-layouts  3.13 us

profile of v1, /device:TPU:1, one launch (start us, length us, event | category | flops | bytes accessed | tf_op | source)
XLA Modules:
  0.0 102.9 jit_solution(11985490699716285978)
XLA Ops:
  0.6 97.8 %exchange.1 = (f32[8,512,128]{2,1,0:T(8,128)}, f32[1,128]{1,0:T(1,128)}) custom-call(f32[16]{0:T(128)} %scale_hbm.1, f32[16]{0:T(128)} %offset_hbm.1, s32[8]{0:T(128)} %scale_index_hbm.1, s32[8]{0:T(128)} %offset_index_hbm.1, f32[8,512,128]{2,1,0:T(8,128)} %bitcast.10, s32[16,512]{1,0:T(8,128)} %bitcast.12), custom_call_target="tpu_custom_call" | custom-call | tf_op jit(solution)/shard_map/exchange/pallas_call | solution.py:345
  98.4 0.8 fusion
  99.2 0.6 pad_maximum_fusion
  99.8 3.1 %copy.10 = f32[8,1,32,2048]{3,2,1,0:T(8,128)} copy(f32[8,1,32,2048]{3,2,1,0:T(8,128)} %bitcast.11) | data formatting | bytes 4194304

commit v2 on v1

--- a/solution.py
+++ b/solution.py
@@ -20,6 +20,8 @@
 OUT_STRIDE = 2 * ROWS * LONS
 STEPS = PLANES // 2
 LAG = 2
+EARLY = 4
+TELL = 6
 STRIDE = 3
 
 def remote(src, dst, send_sem, recv_sem, device):
@@ -32,7 +34,7 @@
 def kernel(
     scale_hbm, offset_hbm, scale_index_hbm, offset_index_hbm, fields, mask,
     out, range_out,
-    scale_table, offset_table, scale_index, offset_index, staged, own_mask, slab_mask, packed, passing, arrived, block, spread_out,
+    scale_table, offset_table, scale_index, offset_index, staged, own_mask, slab_mask, packed, passing, arrived, block, spread_out, highs, lows,
     stat, stat_in, part, part_in, total, range_in,
     load_sem, mask_sem, table_sem, column_send, column_recv,
     send_sem, recv_sem, stat_send, stat_recv, part_send, part_recv, range_send, range_recv, out_sem,
@@ -117,25 +119,22 @@
     for load in loads:
         load.wait()
 
-    def pack(level, carry):
-        base = level * ROWS
-        highest = None
-        lowest = None
-        for k in range(SLOTS):
-            rows = staged[pl.ds(base + chosen[k], FIELDS, stride=FIELD_STRIDE), :]
-            value = (rows - offsets) * scales
-            packed[level, k] = value
-            highest = value if k == 0 else jnp.maximum(highest, value)
-            lowest = value if k == 0 else jnp.minimum(lowest, value)
-        high = jnp.max(highest, axis=1, keepdims=True)
-        low = jnp.max(-lowest, axis=1, keepdims=True)
-        spread = jnp.where(
-            lane == field_row, high, jnp.where(lane == field_row + FIELDS, low, -jnp.inf)
-        )
-        stat[level] = jnp.max(spread, axis=0, keepdims=True)
-        return carry
-
-    lax.fori_loop(0, LEVELS, pack, 0)
+    def pack(turn_, carry):
+        for u in range(4):
+            level = turn_ * 4 + u
+            highest = None
+            lowest = None
+            for k in range(SLOTS):
+                rows = staged[pl.ds(level * ROWS + chosen[k], FIELDS, stride=FIELD_STRIDE), :]
+                value = (rows - offsets) * scales
+                packed[level, k] = value
+                highest = value if k == 0 else jnp.maximum(highest, value)
+                lowest = value if k == 0 else jnp.minimum(lowest, value)
+            highs[level] = highest
+            lows[level] = lowest
+        return carry
+
+    lax.fori_loop(0, LEVELS // 4, pack, 0)
 
     pl.semaphore_wait(barrier, PLANES + SENDERS - 2)
 
@@ -183,6 +182,25 @@
                     source(h), arrived.at[0], send_sem.at[slot, h], recv_sem.at[0], (lat, lon)
                 ).wait_send()
 
+    def start_column(step, carry):
+        both_signs(step, lambda sign: column_copy(step, sign).start())
+        return carry
+
+    lax.fori_loop(0, EARLY, start_column, 0)
+
+    def reduce_stat(turn_, carry):
+        for u in range(4):
+            level = turn_ * 4 + u
+            high = jnp.max(highs[level], axis=1, keepdims=True)
+            low = jnp.max(-lows[level], axis=1, keepdims=True)
+            both = jnp.where(
+                lane == field_row, high, jnp.where(lane == field_row + FIELDS, low, -jnp.inf)
+            )
+            stat[level] = jnp.max(both, axis=0, keepdims=True)
+        return carry
+
+    lax.fori_loop(0, LEVELS // 4, reduce_stat, 0)
+
     def send_stat(k, carry):
         level = lax.rem(me + k, SENDERS)
         remote(
@@ -192,12 +210,6 @@
 
     lax.fori_loop(1, SENDERS, send_stat, 0)
     stat_in[me] = stat[me]
-
-    def start_column(step, carry):
-        both_signs(step, lambda sign: column_copy(step, sign).start())
-        return carry
-
-    lax.fori_loop(0, STEPS, start_column, 0)
     hand_on(lambda h: packed.at[plane * 2 + h], 2 * STEPS, plane)
 
     def take_stat(k, best):
@@ -209,6 +221,8 @@
     part[...] = best
     for k in range(1, PLANES):
         remote(part, part_in.at[k], part_send.at[k], part_recv.at[k], at_plane(k)).start()
+
+    lax.fori_loop(EARLY, STEPS, start_column, 0)
 
     slab_load.wait()
     slab_first = (lon % 4) * 2 * ROWS
@@ -255,7 +269,7 @@
             unpack_step(step - LAG)
         return carry
 
-    lax.fori_loop(0, STEPS, relay, 0)
+    lax.fori_loop(0, TELL, relay, 0)
 
     best = part[...]
     for k in range(1, PLANES):
@@ -283,6 +297,8 @@
         return carry
 
     lax.fori_loop(0, LONS, tell, 0)
+
+    lax.fori_loop(TELL, STEPS, relay, 0)
 
     def unpack_rest(step, carry):
         unpack_step(step)
@@ -302,7 +318,9 @@
     def _():
         remote(total, range_in, range_send.at[0], range_recv, (lat, lon)).wait_recv()
 
-    range_out[...] = range_in[...]
+    ends_row = range_in[...]
+    range_out[0] = ends_row[:, :FIELDS]
+    range_out[1] = -ends_row[:, FIELDS:2 * FIELDS]
 
     def told(q, carry):
         @pl.when(tells & jnp.logical_not(told_self(q)))
@@ -347,7 +365,7 @@
         name="exchange",
         out_shape=(
             jax.ShapeDtypeStruct((FIELDS, OUT_STRIDE, LANES), jnp.float32),
-            jax.ShapeDtypeStruct((1, LANES), jnp.float32),
+            jax.ShapeDtypeStruct((2, 1, FIELDS), jnp.float32),
         ),
         in_specs=[hbm] * 6,
         out_specs=(hbm, vmem),
@@ -362,6 +380,8 @@
             pltpu.VMEM((SENDERS, SLOTS, FIELDS, LANES), jnp.float32),
             pltpu.VMEM((SLOTS, FIELDS, LANES), jnp.float32),
             pltpu.VMEM((FIELDS * OUT_STRIDE, LANES), jnp.float32),
+            pltpu.VMEM((LEVELS, FIELDS, LANES), jnp.float32),
+            pltpu.VMEM((LEVELS, FIELDS, LANES), jnp.float32),
             pltpu.VMEM((LEVELS, 1, LANES), jnp.float32),
             pltpu.VMEM((SENDERS, 1, LANES), jnp.float32),
             pltpu.VMEM((1, LANES), jnp.float32),
@@ -382,7 +402,7 @@
     )
     history = out.reshape(FIELDS, 4, LONS, 8, LANES).transpose(0, 1, 3, 2, 4)
     history = history.reshape(FIELDS, 1, 2 * ROWS, LONS * LANES)
-    record_range = jnp.stack([best[0, :FIELDS], -best[0, FIELDS:2 * FIELDS]])[:, :, None]
+    record_range = best.transpose(0, 2, 1)
     return history, record_range
 
 

time: 104 us -> 102 us (0.981)
  the two profiles are of different devices: /device:TPU:1 before, /device:TPU:2 now
where the time goes in v2:
time: 102 us
  Pallas kernels  97.3 us (95%)
  local copies, waits for them, and re-layouts  3.7 us (4%)
    pallas_call x1, Pallas kernels, per_device(): pl.pallas_call(kernel, name='exchange', out_shape=(jax.ShapeDtypeStruct((...  97.3 us
    unnamed x4, local copies, waits for them, and re-layouts  3.7 us

profile of v2, /device:TPU:2, one launch (start us, length us, event | category | flops | bytes accessed | tf_op | source)
XLA Modules:
  0.0 101.7 jit_solution(1037208069266342781)
XLA Ops:
  0.6 97.3 %exchange.1 = (f32[8,512,128]{2,1,0:T(8,128)}, f32[2,1,8]{2,1,0:T(1,128)}) custom-call(f32[16]{0:T(128)} %scale_hbm.1, f32[16]{0:T(128)} %offset_hbm.1, s32[8]{0:T(128)} %scale_index_hbm.1, s32[8]{0:T(128)} %offset_index_hbm.1, f32[8,512,128]{2,1,0:T(8,128)} %bitcast.10, s32[16,512]{1,0:T(8,128)} %bitcast.12), custom_call_target="tpu_custom_call" | custom-call | tf_op jit(solution)/shard_map/exchange/pallas_call | solution.py:363
  98.0 0.0 copy-start
  98.0 3.1 %copy.11 = f32[8,1,32,2048]{3,2,1,0:T(8,128)} copy(f32[8,1,32,2048]{3,2,1,0:T(8,128)} %bitcast.11) | data formatting | bytes 4194304
  101.1 0.0 copy-done
  101.1 0.6 copy.12
Async XLA Ops:
  98.0 3.1 %copy-start = (f32[2,1,8]{2,1,0:T(1,128)S(1)}, f32[2,1,8]{2,1,0:T(1,128)}, u32[]{:S(2)}) copy-start(f32[2,1,8]{2,1,0:T(1,128)} %get-tuple-element.5) | copy-start | bytes 196
